TPU v7x, 8 devices: a whole 2x2x1 slice. The times are simulated.
8 devices in a mesh: replica: 2 (over z, y), seq: 4 (over x, core).
Axes of the slice: x: 2, y: 2, z: 1, core: 2. Of those that a mesh axis runs over, the one named last changes fastest.
Arguments:
- query_in: bfloat16 [8, 256, 3072], P('replica', 'seq'), parts along dimension 0
- memory: bfloat16 [8, 2048, 3072], P('replica', 'seq'), parts along dimension 0
- mem_len: int32 [8], P('replica'), parts along dimension 0
- w_query: bfloat16 [3072, 16, 256], replicated
- w_key: bfloat16 [3072, 16, 256], replicated
- w_value: bfloat16 [3072, 16, 256], replicated
- w_out: bfloat16 [16, 256, 3072], replicated
Outputs:
- output: bfloat16 [8, 256, 3072], P('replica', 'seq'), parts along dimension 0
There are 2 independent parts. A program takes and returns all parts, laid end to end along the dimension named above; an argument that names none is the same for every part.
All inputs are finite; a program needn't handle non-finite values.
Results may differ from a plain program's by a relative error of at most 0.00767016.
Values are sent between devices in bfloat16 or wider.
A program may use at most 1 GiB of HBM per device.

v0:
```python
import math
import jax
import jax.numpy as jnp
from jax import lax
from jax.sharding import PartitionSpec as P

NEG_BIG = -1e30


def solution(mesh):
    def local_step(query_in, memory, mem_len, w_query, w_key, w_value, w_out):
        n_batch, _, d_model = query_in.shape
        mem_local = memory.shape[1]
        n_heads, head_dim = w_query.shape[1], w_query.shape[2]
        kv_heads = w_key.shape[1]
        group_size = n_heads // kv_heads
        score_scale = 1.0 / math.sqrt(head_dim)
        q_local = jnp.einsum('bsd,dhe->bshe', query_in, w_query, preferred_element_type=jnp.float32).astype(jnp.bfloat16)
        q_all = lax.all_gather(q_local, 'seq', axis=1, tiled=True)
        n_query = q_all.shape[1]
        q_all = q_all.reshape(n_batch, n_query, kv_heads, group_size, head_dim)
        key_loc = jnp.einsum('btd,dke->btke', memory, w_key, preferred_element_type=jnp.float32).astype(jnp.bfloat16)
        val_loc = jnp.einsum('btd,dke->btke', memory, w_value, preferred_element_type=jnp.float32).astype(jnp.bfloat16)
        position = lax.axis_index('seq') * mem_local + jnp.arange(mem_local)
        is_valid = (position[None, :] < mem_len[:, None])[:, None, None, None, :]
        block_cap = 2 ** int(math.log2(max(1, d_model // n_heads)))
        q_block = min(n_query, block_cap)
        max_parts = []
        sum_parts = []
        out_parts = []
        for blk_start in range(0, n_query, q_block):
            q_blk = q_all[:, blk_start:blk_start + q_block]
            scores = jnp.einsum('bqkgd,btkd->bkqgt', q_blk, key_loc, preferred_element_type=jnp.float32) * score_scale
            scores = jnp.where(is_valid, scores, NEG_BIG)
            blk_max = jnp.max(scores, axis=-1)
            weights = jnp.exp(scores - blk_max[..., None])
            max_parts.append(blk_max)
            sum_parts.append(jnp.sum(weights, axis=-1))
            out_parts.append(jnp.einsum('bkqgt,btkd->bkqgd', weights.astype(jnp.bfloat16), val_loc, preferred_element_type=jnp.float32))
        loc_max = jnp.concatenate(max_parts, axis=2)
        loc_sum = jnp.concatenate(sum_parts, axis=2)
        loc_out = jnp.concatenate(out_parts, axis=2)
        glob_max = lax.pmax(loc_max, 'seq')
        factor = jnp.exp(loc_max - glob_max)
        part_stats = jnp.concatenate([loc_out * factor[..., None], (loc_sum * factor)[..., None]], axis=-1)
        combined = lax.psum_scatter(part_stats, 'seq', scatter_dimension=2, tiled=True)
        attended = (combined[..., :head_dim] / combined[..., head_dim:]).astype(jnp.bfloat16)
        w_heads = w_out.reshape(kv_heads, group_size, head_dim, d_model)
        return jnp.einsum('bkqgd,kgde->bqe', attended, w_heads, preferred_element_type=jnp.float32).astype(jnp.bfloat16)

    return jax.shard_map(local_step, mesh=mesh, in_specs=(P('replica', 'seq', None), P('replica', 'seq', None), P('replica'), P(), P(), P(), P()), out_specs=P('replica', 'seq', None), check_vma=False)
```

profile of v0, /device:TPU:0, one launch (start us, length us, event | category | flops | bytes accessed | tf_op | source)
XLA Modules:
  0.0 466.7 jit_solution(12410332644906422480)
XLA Ops:
  6.5 0.0 copy-start
  6.5 0.0 copy-start.4
  6.5 0.0 all-gather.2.cloned.1.call-start
  6.5 1.4 copy-done
  7.9 18.4 %fusion.58 = bf16[4,64,16,256]{3,1,2,0:T(8,128)(2,1)} fusion(bf16[3072,16,256]{2,1,0:T(8,128)(2,1)} %param.10, bf16[4,64,3072]{2,1,0:T(8,128)(2,1)S(1)} %copy-done), kind=kOutput, calls=%fused_computation.49 | convolution fusion | flops 6443499520 | bytes 28835840 | tf_op jit(solution)/shard_map/bsd,dhe->bshe/dot_general | solution.py:18
  26.3 0.0 all-gather.2.cloned.1.call-update
  26.3 0.0 all-reduce.2.cloned.1.call-start
  26.4 0.0 copy-done.4
  26.4 0.7 broadcast_compare_fusion
  27.0 62.2 %fusion.19 = bf16[4,512,16,256]{3,1,2,0:T(8,128)(2,1)} fusion(bf16[3072,16,256]{2,1,0:T(8,128)(2,1)} %param.11, bf16[4,512,3072]{2,1,0:T(8,128)(2,1)} %param.8), kind=kOutput, calls=%fused_computation.25 | convolution fusion | flops 51547996160 | bytes 54525952 | tf_op jit(solution)/shard_map/btd,dke->btke/dot_general | solution.py:22
  89.3 62.1 %fusion.24 = bf16[4,512,16,256]{3,1,2,0:T(8,128)(2,1)} fusion(bf16[3072,16,256]{2,1,0:T(8,128)(2,1)} %param.12, bf16[4,512,3072]{2,1,0:T(8,128)(2,1)} %param.8), kind=kOutput, calls=%fused_computation.26 | convolution fusion | flops 51547996160 | bytes 54525952 | tf_op jit(solution)/shard_map/btd,dke->btke/dot_general | solution.py:23
  151.3 0.0 all-gather.2.cloned.1.call-done
  151.4 0.0 copy-done.3
  151.4 13.1 %fusion.11 = (f32[4,16,128]{2,1,0:T(8,128)S(1)}, f32[4,16,128,512]{3,2,1,0:T(8,128)}) fusion(pred[4,512]{1,0:T(4,128)(4,1)S(1)} %copy-done.3, bf16[4,512,16,256]{3,1,2,0:T(8,128)(2,1)} %fusion.19, bf16[4,256,16,1,256]{4,1,2,0,3:T(8,128)(2,1)} %bitcast.73), kind=kOutput, calls=%fused_computation.17 | convolution fusion | flops 2160058368 | bytes 37783552 | tf_op jit(solution)/shard_map/bqkgd,btkd->bkqgt/dot_general | solution.py:33
  164.5 20.0 %fusion.13 = (f32[4,16,128]{2,1,0:T(8,128)S(1)}, f32[4,16,128]{2,1,0:T(8,128)S(1)}, f32[4,16,128,512]{3,2,1,0:T(8,128)}) fusion(f32[4,16,128,512]{3,2,1,0:T(8,128)} %get-tuple-element.10, f32[4,16,128]{2,1,0:T(8,128)S(1)} %get-tuple-element.9, pred[4,512]{1,0:T(4,128)(4,1)S(1)} %copy-done.3, bf16[4,512,16,256]{3,1,2,0:T(8,128)(2,1)} %fusion.19, ...), kind=kOutput, calls=%fused_computation.19 | convolution fusion | flops 2176827392 | bytes 54626304 | tf_op jit(solution)/shard_map/bqkgd,btkd->bkqgt/dot_general | solution.py:33
  184.5 17.5 %fusion.50 = f32[4,16,128,1,256]{4,2,1,0,3:T(8,128)} fusion(bf16[4,512,16,256]{3,1,2,0:T(8,128)(2,1)} %fusion.24, f32[4,16,128,512]{3,2,1,0:T(8,128)} %get-tuple-element.10, f32[4,16,128]{2,1,0:T(8,128)S(1)} %get-tuple-element.9, pred[4,512]{1,0:T(4,128)(4,1)S(1)} %copy-done.3), kind=kOutput, calls=%fused_computation.45 | convolution fusion | flops 2164260864 | bytes 41977856 | tf_op jit(solution)/shard_map/bkqgt,btkd->bkqgd/dot_general | solution.py:39
  202.0 17.6 %fusion.53 = f32[4,16,128,1,256]{4,2,1,0,3:T(8,128)} fusion(bf16[4,512,16,256]{3,1,2,0:T(8,128)(2,1)} %fusion.24, f32[4,16,128,512]{3,2,1,0:T(8,128)} %get-tuple-element.11, f32[4,16,128]{2,1,0:T(8,128)S(1)} %get-tuple-element.6, pred[4,512]{1,0:T(4,128)(4,1)S(1)} %copy-done.3), kind=kOutput, calls=%fused_computation.46 | convolution fusion | flops 2164260864 | bytes 41977856 | tf_op jit(solution)/shard_map/bkqgt,btkd->bkqgd/dot_general | solution.py:39
  219.6 0.6 pad_maximum_fusion.1
  220.2 0.0 all-reduce.2.cloned.1.call-update
  220.2 0.0 reduce-scatter.2.cloned.1.call-start
  220.3 8.2 %fusion.15 = f32[4,16,128]{2,1,0:T(8,128)S(1)} fusion(f32[4,16,128,512]{3,2,1,0:T(8,128)} %get-tuple-element.11, f32[4,16,128]{2,1,0:T(8,128)S(1)} %get-tuple-element.6, pred[4,512]{1,0:T(4,128)(4,1)S(1)} %copy-done.3), kind=kLoop, calls=%fused_computation.21 | loop fusion | flops 16769024 | bytes 16844800 | tf_op jit(solution)/shard_map/reduce_sum | solution.py:38
  228.5 20.7 %all-reduce.2.cloned.1.call-done = f32[4,16,256,1]{2,1,0,3:T(8,128)} async-done(((f32[4,16,256,1]{2,1,0,3:T(8,128)}), f32[4,16,256,1]{2,1,0,3:T(8,128)}) %all-reduce.2.cloned.1.call-update) | async-done | bytes 65552 | tf_op jit(solution)/shard_map/pmax | solution.py:43
  249.1 0.9 fusion.63
  250.0 4.7 copy.14
  254.7 7.3 %maximum_multiply_fusion = f32[4,16,256,1,256]{4,2,1,0,3:T(8,128)S(1)} fusion(f32[4,16,128,1,256]{4,2,1,0,3:T(8,128)} %fusion.53, f32[4,16,128,1,256]{4,2,1,0,3:T(8,128)} %fusion.50, f32[4,16,256]{2,1,0:T(8,128)S(1)} %get-tuple-element.7), kind=kLoop, calls=%fused_computation.12 | loop fusion | flops 8388608 | bytes 33619968 | tf_op jit(solution)/shard_map/mul | solution.py:45
  262.0 0.9 copy-done.2
  262.9 8.7 %pad_maximum_fusion = f32[4,16,256,1,257]{4,2,1,0,3:T(8,128)} fusion(f32[4,16,256,1,1]{4,2,1,0,3:T(8,128)S(1)} %copy-done.2, f32[4,16,256,1,256]{4,2,1,0,3:T(8,128)S(1)} %maximum_multiply_fusion), kind=kLoop, calls=%fused_computation | loop fusion | flops 4210688 | bytes 33685504 | tf_op jit(solution)/shard_map/concatenate | solution.py:45
  271.6 0.0 reduce-scatter.2.cloned.1.call-update
  271.6 169.2 %reduce-scatter.2.cloned.1.call-done = f32[4,16,64,1,257]{4,2,1,0,3:T(8,128)} async-done(((f32[4,16,256,1,257]{4,2,1,0,3:T(8,128)}), f32[4,16,64,1,257]{4,2,1,0,3:T(8,128)}) %reduce-scatter.2.cloned.1.call-update) | async-done | bytes 4210704 | tf_op jit(solution)/shard_map/reduce_scatter | solution.py:46
  440.9 2.3 slice_reduce_fusion
  443.2 16.7 %fusion.47 = bf16[4,64,3072]{2,1,0:T(8,128)(2,1)} fusion(bf16[16,256,3072]{2,1,0:T(8,128)(2,1)} %param.13, f32[4,16,64,1,257]{4,2,1,0,3:T(8,128)} %reduce-scatter.2.cloned.1.call-done, f32[4,16,64]{2,1,0:T(8,128)S(1)} %slice_reduce_fusion), kind=kOutput, calls=%fused_computation.44 | convolution fusion | flops 6445334528 | bytes 30949376 | tf_op jit(solution)/shard_map/bkqgd,kgde->bqe/dot_general | solution.py:49
  459.9 0.0 copy-done.1
  (4 shorter events, 0.0 us)
Async XLA Ops:
  6.5 1.4 copy-start
  6.5 19.9 %copy-start.4 = (s32[4]{0:T(128)S(1)}, s32[4]{0:T(128)}, u32[]{:S(2)}) copy-start(s32[4]{0:T(128)} %param.9) | copy-start | bytes 52
  6.5 144.8 %all-gather.2.cloned.1.call-start = ((), (), s32[]{:S(2)}) async-start(), calls=%async_computation.1 | async-start | bytes 10485760 | tf_op jit(solution)/shard_map/all_gather | solution.py:19
  26.3 222.8 %all-reduce.2.cloned.1.call-start = ((), (), s32[]{:S(2)}) async-start(), calls=%async_computation.2 | async-start | bytes 131072 | tf_op jit(solution)/shard_map/pmax | solution.py:43
  89.3 62.1 %copy-start.3 = (pred[4,512]{1,0:T(4,128)(4,1)S(1)}, pred[4,512]{1,0:T(4,128)(4,1)}, u32[]{:S(2)}) copy-start(pred[4,512]{1,0:T(4,128)(4,1)} %broadcast_compare_fusion) | copy-start | bytes 6148
  220.2 220.6 %reduce-scatter.2.cloned.1.call-start = ((), (), s32[]{:S(2)}) async-start(), calls=%async_computation.3 | async-start | bytes 31457280 | tf_op jit(solution)/shard_map/reduce_scatter | solution.py:46
  254.7 8.2 %copy-start.2 = (f32[4,16,256,1,1]{4,2,1,0,3:T(8,128)S(1)}, f32[4,16,256,1,1]{4,2,1,0,3:T(8,128)}, u32[]{:S(2)}) copy-start(f32[4,16,256,1,1]{4,2,1,0,3:T(8,128)} %copy.14) | copy-start | bytes 196612
  440.9 19.1 %copy-start.1 = (bf16[4,64,3072]{2,1,0:T(8,128)(2,1)S(1)}, bf16[4,64,3072]{2,1,0:T(8,128)(2,1)}, u32[]{:S(2)}) copy-start(bf16[4,64,3072]{2,1,0:T(8,128)(2,1)} %param.7) | copy-start | bytes 4718596
Sparse Core Ops, SparseCore 0:
  26.4 58.5 all-gather.1
  220.3 28.7 all-reduce.1
  271.7 169.0 reduce-scatter.1
where the time goes:
time: 471 us; the launch traced here: 467 us
  matrix products  228 us (48%)
  waiting for transfers between devices  190 us (40%)
  other arithmetic  26.4 us (6%)
  between operations  13.4 us (3%)
  local copies, waits for them, and re-layouts  9.33 us (2%)
    reduce_scatter x1, waiting for transfers between devices, local_step(): lax.psum_scatter(part_stats, 'seq', scatter_dimension=2, tiled=True)  169 us
    dot_general x1, matrix products, local_step(): jnp.einsum('btd,dke->btke', memory, w_key, preferred_element_type=jnp.flo...  62.2 us
    dot_general x1, matrix products, local_step(): jnp.einsum('btd,dke->btke', memory, w_value, preferred_element_type=jnp.f...  62.1 us
    dot_general x2, matrix products, local_step(): jnp.einsum('bkqgt,btkd->bkqgd', weights.astype(jnp.bfloat16), val_loc, pr...  35.1 us
    dot_general x2, matrix products, local_step(): jnp.einsum('bqkgd,btkd->bkqgt', q_blk, key_loc, preferred_element_type=jn...  33.1 us
    pmax x1, waiting for transfers between devices, local_step(): glob_max = lax.pmax(loc_max, 'seq')  20.7 us
    dot_general x1, matrix products, local_step(): jnp.einsum('bsd,dhe->bshe', query_in, w_query, preferred_element_type=jnp...  18.4 us
    dot_general x1, matrix products, local_step(): jnp.einsum('bkqgd,kgde->bqe', attended, w_heads, preferred_element_type=j...  16.7 us
  transfers between devices with their start and end apart: 3, of which 2 were waited for; matrix products, arithmetic and copies ran while one was open for 29% of the time, Pallas kernels for 0%

commit v1 on v0

v1 whole, which is shorter than its diff:
```python
import functools
import math
import jax
import jax.numpy as jnp
from jax import lax
from jax.experimental import pallas as pl
from jax.experimental.pallas import tpu as pltpu
from jax.sharding import PartitionSpec as P

NEG_BIG = -1e30
BF16 = jnp.bfloat16
F32 = jnp.float32


def attend_kernel(len_ref, qin_hbm, mem_hbm, wq_hbm, wk_hbm, wv_hbm, wo_hbm,
                  out_hbm, oown_hbm, orecv_hbm, qown_hbm, qrecv_hbm,
                  x_buf, q_in, q_buf, raw_k, raw_v, w_a, w_b, kv_a, kv_b, o_buf, s_buf, s_recv,
                  c_rx, att_tx, out_buf, acc_buf,
                  x_sem, xr_send, xr_recv, qi_sem, qi_send, qi_recv, raw_sem,
                  q_send, q_recv, ql_sem, o_ssem, o_rsem, s_ssem, s_rsem, oo_sem,
                  wo_sem, c_sem, a_ssem, a_rsem, out_sem, free_sem):
    me = lax.axis_index('seq')
    chip = me // 2
    core = lax.rem(me, 2)
    partner = 2 * chip + (1 - core)
    cross = 2 * (1 - chip) + core
    n_batch, rows, d_model = mem_hbm.shape
    q_loc = qin_hbm.shape[1]
    head_dim = wq_hbm.shape[2]
    n_heads = wq_hbm.shape[1] // 2
    n_pairs = n_heads // 2
    head0 = core * n_heads
    half_q = 2 * q_loc
    n_q = n_batch * half_q
    per_att = d_model // head_dim
    scale = 1.0 / math.sqrt(head_dim)

    def to(dev):
        return dict(device_id={'seq': dev}, device_id_type=pl.DeviceIdType.MESH)

    def raw_copy(src, pair, k):
        return pltpu.make_async_copy(src.at[:, pl.ds(head0 + 2 * pair, 2), :], (raw_k, raw_v)[k], raw_sem.at[k])

    def x_local(b):
        return pltpu.make_async_copy(mem_hbm.at[b], x_buf.at[core, pl.ds(b * rows, rows)], x_sem.at[b])

    def x_remote(b):
        return pltpu.make_async_remote_copy(
            mem_hbm.at[b], x_buf.at[core, pl.ds(b * rows, rows)], xr_send.at[b], xr_recv.at[b], **to(partner))

    def q_copy(pair):
        sl = pl.ds(2 * pair, 2)
        return pltpu.make_async_remote_copy(qown_hbm.at[sl], qrecv_hbm.at[sl], q_send.at[pair], q_recv.at[pair], **to(cross))

    def q_store(pair):
        return pltpu.make_async_copy(q_buf.at[pair % 2], qown_hbm.at[pl.ds(2 * pair, 2)], ql_sem.at[pair % 2, 0])

    def q_loads(h, k):
        return (pltpu.make_async_copy(qown_hbm.at[h], q_buf.at[k, 0], ql_sem.at[k, 0]),
                pltpu.make_async_copy(qrecv_hbm.at[h], q_buf.at[k, 1], ql_sem.at[k, 1]))

    def o_copy(h, k):
        return pltpu.make_async_remote_copy(o_buf.at[k, 1], orecv_hbm.at[h], o_ssem.at[k], o_rsem.at[h], **to(cross))

    def o_piece(h, k, b):
        r = pl.ds(pl.multiple_of(b * half_q, half_q), half_q)
        return pltpu.make_async_remote_copy(o_buf.at[k, 1, r], orecv_hbm.at[h, r], o_ssem.at[k], o_rsem.at[h], **to(cross))

    def s_copy(h, k):
        return pltpu.make_async_remote_copy(s_buf.at[h, 1], s_recv.at[h], s_ssem.at[k], s_rsem.at[h], **to(cross))

    def oo_copy(h, k):
        return pltpu.make_async_copy(o_buf.at[k, 0], oown_hbm.at[h], oo_sem.at[k])

    qi_local = pltpu.make_async_copy(qin_hbm, q_in.at[:, core], qi_sem)
    raw_copy(wq_hbm, 0, 0).start()
    raw_copy(wq_hbm, 1, 1).start()
    qi_local.start()
    for b in range(n_batch):
        x_local(b).start()

    barrier = pltpu.get_barrier_semaphore()
    pl.semaphore_signal(barrier, inc=1, **to(partner))
    pl.semaphore_signal(barrier, inc=1, **to(cross))
    pl.semaphore_wait(barrier, 2)

    qi_remote = pltpu.make_async_remote_copy(qin_hbm, q_in.at[:, core], qi_send, qi_recv, **to(partner))
    qi_remote.start()
    for b in range(n_batch):
        x_remote(b).start()

    step = 128

    def relayout(raw, dst, sel, start, size):
        for i in range(size // step):
            r = pl.ds(pl.multiple_of(start + i * step, step), step)
            t = jnp.swapaxes(raw[r], 0, 1)
            dst[0, sel, r, :] = t[0]
            dst[1, sel, r, :] = t[1]

    half = d_model // 2

    raw_copy(wq_hbm, 0, 0).wait()

    def first_q(i, carry):
        relayout(raw_k, w_b, 0, i * half, half)
        return carry

    lax.fori_loop(0, 2, first_q, 0)
    raw_copy(wq_hbm, 2, 0).start()
    qi_local.wait()
    qi_remote.wait()
    for pair in range(n_pairs):
        k = (pair + 1) % 2
        last = pair + 1 == n_pairs
        src, idx = (wk_hbm, 0) if last else (wq_hbm, pair + 1)
        raw_copy(src, idx, k).wait()

        if pair >= 2:
            q_store(pair - 2).wait()
            q_copy(pair - 2).start()

        def q_step(j, carry, pair=pair, k=k, last=last):
            relayout((raw_k, raw_v)[k], w_a if last else w_b, 0 if last else k, j * half, half)
            q_rows = q_in[...].reshape(n_q, d_model)
            res = jnp.dot(q_rows, w_b[j, pair % 2], preferred_element_type=F32)
            q_buf[pair % 2, j] = res.astype(BF16)
            return carry

        lax.fori_loop(0, 2, q_step, 0)
        q_store(pair).start()
        if pair + 3 < n_pairs:
            raw_copy(wq_hbm, pair + 3, k).start()
        elif pair + 3 == n_pairs:
            raw_copy(wk_hbm, 0, k).start()
        elif pair + 2 == n_pairs:
            raw_copy(wv_hbm, 0, k).start()
    pl.semaphore_signal(free_sem, inc=1, **to(partner))
    raw_copy(wk_hbm, 1, 0).start()
    for pair in (n_pairs - 2, n_pairs - 1):
        q_store(pair).wait()
        q_copy(pair).start()
    raw_copy(wv_hbm, 0, 1).wait()

    def first_v(i, carry):
        relayout(raw_v, w_a, 1, i * half, half)
        return carry

    lax.fori_loop(0, 2, first_v, 0)
    raw_copy(wv_hbm, 1, 1).start()
    for b in range(n_batch):
        x_local(b).wait()

    def slices(b):
        return (pl.ds(pl.multiple_of(b * half_q, half_q), half_q), pl.ds(pl.multiple_of(b * rows, rows), rows))

    def weights(h, b, side, kv, k):
        q_sl, kv_sl = slices(b)
        k_b = kv[0, :, kv_sl, :].reshape(2 * rows, head_dim)
        s = lax.dot_general(q_buf[k, side, q_sl, :], k_b, (((1,), (1,)), ((), ())), preferred_element_type=F32) * scale
        pos = lax.broadcasted_iota(jnp.int32, s.shape, 1)
        s = jnp.where(pos < len_ref[b] - chip * (2 * rows), s, NEG_BIG)
        m = jnp.max(s, axis=1, keepdims=True)
        p = jnp.exp(s - m)
        l = jnp.sum(p, axis=1, keepdims=True)
        lane = lax.broadcasted_iota(jnp.int32, (half_q, 128), 1)
        s_buf[h, side, :, q_sl] = jnp.where(lane == 0, m, l).T[0:8]
        return p.astype(BF16)

    def weighted(p, b, side, kv, k):
        q_sl, kv_sl = slices(b)
        v_b = kv[1, :, kv_sl, :].reshape(2 * rows, head_dim)
        o_buf[k, side, q_sl, :] = jnp.dot(p, v_b, preferred_element_type=F32)

    n_tiles = 2 * n_batch
    part = d_model // n_batch
    big = n_batch * rows // 2

    def four_heads(sp, carry):
        for u in range(4):
            h = 4 * sp + u
            pair = 2 * sp + u // 2
            j = u % 2
            w_now, w_next = (w_a, w_b) if u < 2 else (w_b, w_a)
            kv_now, kv_prev = (kv_a, kv_b) if j == 0 else (kv_b, kv_a)
            k_prev = (u + 1) % 2
            h_prev = jnp.maximum(h - 1, 0)

            @pl.when(h >= 3)
            def _():
                o_copy(h - 3, k_prev).wait_send()
                s_copy(h - 3, k_prev).wait_send()
                oo_copy(h - 3, k_prev).wait()

            @pl.when(pair + 1 < n_pairs)
            def _(j=j, pair=pair):
                raw_copy((wk_hbm, wv_hbm)[j], pair + 1, j).wait()

            @pl.when(h >= 1)
            def _():
                for c in q_loads(h_prev, k_prev):
                    c.wait()

            def fetch_q(h=h, pair=pair, j=j):
                if j == 0:
                    q_copy(pair).wait()
                for c in q_loads(h, j):
                    c.start()

            if u == 0:
                pl.when(h >= 1)(fetch_q)
            else:
                fetch_q()

            def tile(t, c, fetch_q=fetch_q, u=u, h=h, j=j, w_now=w_now, w_next=w_next, kv_now=kv_now, kv_prev=kv_prev, k_prev=k_prev, h_prev=h_prev):
                if u == 0:
                    @pl.when((h == 0) & (t == n_batch // 2))
                    def _():
                        for b in range(n_batch):
                            x_remote(b).wait()
                        fetch_q()

                relayout((raw_k, raw_v)[j], w_next, j, t * part, part)
                p = [weights(h_prev, t, i, kv_prev, k_prev) for i in range(2)]
                side = lax.rem(core + t // 2, 2)
                r = pl.ds(pl.multiple_of(lax.rem(t, 2) * big, big), big)
                for sel in range(2):
                    kv_now[sel, side, r, :] = jnp.dot(x_buf[side, r, :], w_now[j, sel], preferred_element_type=F32).astype(BF16)
                    weighted(p[sel], t, sel, kv_prev, k_prev)

                @pl.when(h >= 1)
                def _():
                    o_piece(h - 1, k_prev, t).start()

                return c

            lax.fori_loop(0, n_batch, tile, 0)

            @pl.when(pair + 2 < n_pairs)
            def _(j=j, pair=pair):
                raw_copy((wk_hbm, wv_hbm)[j], pair + 2, j).start()

            @pl.when(h >= 1)
            def _():
                s_copy(h - 1, k_prev).start()
                oo_copy(h - 1, k_prev).start()
        return carry

    lax.fori_loop(0, n_heads // 4, four_heads, 0)

    n_wo = wo_hbm.shape[0] // 2
    wo_copies = [pltpu.make_async_copy(wo_hbm.at[pl.ds(i * n_wo, n_wo)], x_buf.at[i], wo_sem.at[i]) for i in range(2)]
    for c in wo_copies:
        c.start()

    final = n_heads - 1
    o_copy(final - 2, 1).wait_send()
    s_copy(final - 2, 1).wait_send()
    oo_copy(final - 2, 1).wait()

    for c in q_loads(final, 1):
        c.wait()

    def last_attention(b, c, side):
        weighted(weights(final, b, side, kv_b, 1), b, side, kv_b, 1)
        if side == 1:
            o_piece(final, 1, b).start()
        return c

    lax.fori_loop(0, n_batch, functools.partial(last_attention, side=1), 0)
    s_copy(final, 1).start()
    lax.fori_loop(0, n_batch, functools.partial(last_attention, side=0), 0)
    oo_copy(final, 1).start()

    half_rows = n_q // 2
    n_half = n_batch // 2

    def c_copies(h, i):
        r = pl.ds(i * half_rows, half_rows)
        return (pltpu.make_async_copy(oown_hbm.at[h, r], o_buf.at[0, 0, r], c_sem.at[0, i]),
                pltpu.make_async_copy(orecv_hbm.at[h, r], c_rx.at[i], c_sem.at[1, i]))

    def att_slot(h):
        hg = head0 + h
        return hg // per_att, pl.ds(pl.multiple_of(lax.rem(hg, per_att) * head_dim, head_dim), head_dim)

    def a_copy(h, k):
        side, lanes = att_slot(h)
        return pltpu.make_async_remote_copy(att_tx.at[k], q_in.at[:, side, :, lanes], a_ssem.at[k], a_rsem.at[h], **to(partner))

    def combine(h, k, following):
        t1, t2 = s_buf[h, 0].T, s_recv[h].T
        m1, l1, m2, l2 = t1[:, 0:1], t1[:, 1:2], t2[:, 0:1], t2[:, 1:2]
        m = jnp.maximum(m1, m2)
        f1, f2 = jnp.exp(m1 - m), jnp.exp(m2 - m)
        den = l1 * f1 + l2 * f2
        f1, f2 = f1 / den, f2 / den
        side, lanes = att_slot(h)
        for i in range(2):
            for c in c_copies(h, i):
                c.wait()
            for b in range(i * n_half, (i + 1) * n_half):
                r = slice(b * half_q, (b + 1) * half_q)
                rc = slice((b - i * n_half) * half_q, (b - i * n_half + 1) * half_q)
                res = (o_buf[0, 0, r, :] * f1[r] + c_rx[i, rc, :] * f2[r]).astype(BF16)
                lo, hi = res[:q_loc], res[q_loc:]
                q_in[b, side, :, lanes] = jnp.where(core == 0, lo, hi)
                att_tx[k, b] = jnp.where(core == 0, hi, lo)
            following(i)

    oo_copy(final - 1, 0).wait()
    o_copy(final - 1, 0).wait_send()
    s_copy(final - 1, 0).wait_send()
    pl.semaphore_wait(free_sem, 1)
    o_copy(0, 0).wait_recv()
    s_copy(0, 0).wait_recv()
    for i in range(2):
        for c in c_copies(0, i):
            c.start()

    def combine_step(h, carry):
        k = lax.rem(h, 2)

        @pl.when(h + 1 < final)
        def _():
            o_copy(h + 1, 0).wait_recv()
            s_copy(h + 1, 0).wait_recv()

        @pl.when(h >= 2)
        def _():
            a_copy(h - 2, k).wait_send()

        def following(i):
            @pl.when(h + 1 < final)
            def _():
                for c in c_copies(h + 1, i):
                    c.start()

        combine(h, k, following)
        a_copy(h, k).start()
        return carry

    lax.fori_loop(0, final, combine_step, 0)
    for c in wo_copies:
        c.wait()
    for h in range(final):
        a_copy(h, 0).wait_recv()

    width = out_buf.shape[2]
    n_out = n_batch * q_loc
    most = final * head_dim
    rest = 2 * n_wo - d_model
    n_cols = d_model // width

    def columns(n):
        return pl.ds(pl.multiple_of(n * width, width), width)

    def early_tile(n, carry):
        cols = columns(n)
        acc = jnp.dot(q_in[:, 0, :, 0:most].reshape(n_out, most), x_buf[0, 0:most, cols], preferred_element_type=F32)
        acc += jnp.dot(q_in[:, 0, :, n_wo:].reshape(n_out, d_model - n_wo), x_buf[1, 0:d_model - n_wo, cols], preferred_element_type=F32)
        acc += jnp.dot(q_in[:, 1, :, 0:rest - head_dim].reshape(n_out, rest - head_dim), x_buf[1, d_model - n_wo:most, cols], preferred_element_type=F32)
        acc_buf[:, cols] = acc
        return carry

    lax.fori_loop(0, n_cols, early_tile, 0)
    k = final % 2
    oo_copy(final, 1).wait()
    o_copy(final, 1).wait_send()
    s_copy(final, 1).wait_send()
    a_copy(final - 2, k).wait_send()
    o_copy(final, 1).wait_recv()
    s_copy(final, 1).wait_recv()
    for i in range(2):
        for c in c_copies(final, i):
            c.start()
    combine(final, k, lambda i: None)
    a_copy(final, k).start()
    a_copy(final - 1, 1 - k).wait_send()
    a_copy(final, k).wait_send()
    a_copy(final, k).wait_recv()

    def out_copy(n, k):
        return pltpu.make_async_copy(out_buf.at[k], out_hbm.at[:, columns(n)], out_sem.at[k])

    def out_tile(n, carry):
        k = lax.rem(n, 2)

        @pl.when(n >= 2)
        def _():
            out_copy(n - 2, k).wait()

        cols = columns(n)
        acc = acc_buf[:, cols] + jnp.dot(q_in[:, 0, :, most:n_wo].reshape(n_out, head_dim), x_buf[0, most:n_wo, cols], preferred_element_type=F32)
        acc += jnp.dot(q_in[:, 1, :, rest - head_dim:rest].reshape(n_out, head_dim), x_buf[1, most:n_wo, cols], preferred_element_type=F32)
        out_buf[k] = acc.astype(BF16)
        out_copy(n, k).start()
        return carry

    lax.fori_loop(0, n_cols, out_tile, 0)
    for n in (n_cols - 2, n_cols - 1):
        out_copy(n, n % 2).wait()


def solution(mesh):
    def local_step(query_in, memory, mem_len, w_query, w_key, w_value, w_out):
        n_batch, q_loc, d_model = query_in.shape
        mem_local = memory.shape[1]
        head_dim = w_query.shape[2]
        n_heads = w_query.shape[1] // 2
        n_pairs = n_heads // 2
        n_q = n_batch * 2 * q_loc
        out_width = 512
        any_spec = pl.BlockSpec(memory_space=pl.ANY)
        part = jax.ShapeDtypeStruct((n_heads, n_q, head_dim), F32)
        dma = pltpu.SemaphoreType.DMA
        q_part = jax.ShapeDtypeStruct((n_heads, n_q, head_dim), BF16)
        out = pl.pallas_call(
            attend_kernel,
            out_shape=(jax.ShapeDtypeStruct((n_batch * q_loc, d_model), BF16), part, part, q_part, q_part),
            in_specs=[pl.BlockSpec(memory_space=pltpu.SMEM)] + [any_spec] * 6,
            out_specs=(any_spec,) * 5,
            scratch_shapes=[
                pltpu.VMEM((2, n_batch * mem_local, d_model), BF16),
                pltpu.VMEM((n_batch, 2, q_loc, d_model), BF16),
                pltpu.VMEM((2, 2, n_q, head_dim), BF16),
                pltpu.VMEM((d_model, 2, head_dim), BF16),
                pltpu.VMEM((d_model, 2, head_dim), BF16),
                pltpu.VMEM((2, 2, d_model, head_dim), BF16),
                pltpu.VMEM((2, 2, d_model, head_dim), BF16),
                pltpu.VMEM((2, 2, n_batch * mem_local, head_dim), BF16),
                pltpu.VMEM((2, 2, n_batch * mem_local, head_dim), BF16),
                pltpu.VMEM((2, 2, n_q, head_dim), F32),
                pltpu.VMEM((n_heads, 2, 8, n_q), F32),
                pltpu.VMEM((n_heads, 8, n_q), F32),
                pltpu.VMEM((2, n_q // 2, head_dim), F32),
                pltpu.VMEM((2, n_batch, q_loc, head_dim), BF16),
                pltpu.VMEM((2, n_batch * q_loc, out_width), BF16),
                pltpu.VMEM((n_batch * q_loc, d_model), F32),
                dma((n_batch,)), dma((n_batch,)), dma((n_batch,)), dma, dma, dma, dma((2,)),
                dma((n_pairs,)), dma((n_pairs,)), dma((2, 2)), dma((2,)), dma((n_heads,)), dma((2,)), dma((n_heads,)), dma((2,)),
                dma((2,)), dma((2, 2)), dma((2,)), dma((n_heads,)), dma((2,)), pltpu.SemaphoreType.REGULAR,
            ],
            compiler_params=pltpu.CompilerParams(collective_id=0, has_side_effects=True, vmem_limit_bytes=67043328),
        )(mem_len, query_in, memory, w_query, w_key, w_value, w_out.reshape(2 * n_heads * head_dim, d_model))[0]
        return out.reshape(n_batch, q_loc, d_model)

    return jax.shard_map(local_step, mesh=mesh, in_specs=(P('replica', 'seq', None), P('replica', 'seq', None), P('replica'), P(), P(), P(), P()), out_specs=P('replica', 'seq', None), check_vma=False)
```

time: 471 us -> 197 us (0.42)
  matrix products: 228 us -> 0 us
  Pallas kernels: 0 us -> 194 us
  waiting for transfers between devices: 190 us -> 0 us
  other arithmetic: 26.4 us -> 0 us
  between operations: 13.4 us -> 0.01 us
  local copies, waits for them, and re-layouts: 9.33 us -> 2.65 us
    dot_general x8 -> x0, matrix products: 228 us -> none  [the longest x1 62.2 us: local_step(): jnp.einsum('btd,dke->btke', memory, w_key, preferred_element_type=jnp.flo...]
    pallas_call x0 -> x1, Pallas kernels: none -> 194 us  [local_step(): pl.pallas_call(attend_kernel, out_shape=(jax.ShapeDtypeStruct((n_batch *...]
    reduce_scatter x1 -> x0, waiting for transfers between devices: 169 us -> none  [local_step(): lax.psum_scatter(part_stats, 'seq', scatter_dimension=2, tiled=True)]
    pmax x1 -> x0, waiting for transfers between devices: 20.7 us -> none  [local_step(): glob_max = lax.pmax(loc_max, 'seq')]
    concatenate x2 -> x0, other arithmetic: 9.31 us -> none  [the longest x1 8.68 us: local_step(): jnp.concatenate([loc_out * factor[..., None], (loc_sum * factor)[..., Non...]
    reduce_sum x1 -> x0, other arithmetic: 8.21 us -> none  [local_step(): sum_parts.append(jnp.sum(weights, axis=-1))]
    mul x2 -> x0, other arithmetic: 8.17 us -> none  [local_step(): loc_out * factor[..., None]]
  transfers between devices with their start and end apart: 3 -> 0, of which waited for: 2 -> 0; matrix products, arithmetic and copies ran while one was open for 29% -> 0% of each run, Pallas kernels for 0% -> 0%
where the time goes in v1:
time: 197 us; the launch traced here: 196 us
  Pallas kernels  194 us (98%)
  local copies, waits for them, and re-layouts  2.65 us (1%)
    pallas_call x1, Pallas kernels, local_step(): pl.pallas_call(attend_kernel, out_shape=(jax.ShapeDtypeStruct((n_batch *...  194 us

profile of v1, /device:TPU:0, one launch (start us, length us, event | category | flops | bytes accessed | tf_op | source)
XLA Modules:
  0.0 196.3 jit_solution(10894626897696594387)
XLA Ops:
  0.0 193.6 %shard_map.73 = (bf16[256,3072]{1,0:T(8,128)(2,1)}, f32[8,512,256]{2,1,0:T(8,128)}, f32[8,512,256]{2,1,0:T(8,128)}, bf16[8,512,256]{2,1,0:T(8,128)(2,1)}, bf16[8,512,256]{2,1,0:T(8,128)(2,1)}) custom-call(s32[4]{0:T(128)} %len_ref.1, bf16[4,64,3072]{2,1,0:T(8,128)(2,1)} %qin_hbm.1, bf16[4,512,3072]{2,1,0:T(8,128)(2,1)} %mem_hbm.1, ...), custom_call_target="tpu_custom_call" | custom-call | tf_op jit(solution)/shard_map/pallas_call | solution.py:418
  193.6 2.7 %copy.9 = bf16[4,64,3072]{2,1,0:T(8,128)(2,1)} copy(bf16[4,64,3072]{2,1,0:T(8,128)(2,1)} %bitcast.3) | data formatting | bytes 3145728

commit v2 on v1

--- a/solution.py
+++ b/solution.py
@@ -120,13 +120,17 @@
             q_store(pair - 2).wait()
             q_copy(pair - 2).start()
 
-        def q_step(j, carry, pair=pair, k=k, last=last):
+        def q_next(j, carry, k=k, last=last):
             relayout((raw_k, raw_v)[k], w_a if last else w_b, 0 if last else k, j * half, half)
+            return carry
+
+        def q_step(j, carry, pair=pair):
             q_rows = q_in[...].reshape(n_q, d_model)
             res = jnp.dot(q_rows, w_b[j, pair % 2], preferred_element_type=F32)
             q_buf[pair % 2, j] = res.astype(BF16)
             return carry
 
+        lax.fori_loop(0, 2, q_next, 0)
         lax.fori_loop(0, 2, q_step, 0)
         q_store(pair).start()
         if pair + 3 < n_pairs:
@@ -212,7 +216,7 @@
             else:
                 fetch_q()
 
-            def tile(t, c, fetch_q=fetch_q, u=u, h=h, j=j, w_now=w_now, w_next=w_next, kv_now=kv_now, kv_prev=kv_prev, k_prev=k_prev, h_prev=h_prev):
+            def tile(t, c, fetch_q=fetch_q, pair=pair, u=u, h=h, j=j, w_now=w_now, w_next=w_next, kv_now=kv_now, kv_prev=kv_prev, k_prev=k_prev, h_prev=h_prev):
                 if u == 0:
                     @pl.when((h == 0) & (t == n_batch // 2))
                     def _():
@@ -220,7 +224,10 @@
                             x_remote(b).wait()
                         fetch_q()
 
-                relayout((raw_k, raw_v)[j], w_next, j, t * part, part)
+                @pl.when(pair + 1 < n_pairs)
+                def _():
+                    relayout((raw_k, raw_v)[j], w_next, j, t * part, part)
+
                 p = [weights(h_prev, t, i, kv_prev, k_prev) for i in range(2)]
                 side = lax.rem(core + t // 2, 2)
                 r = pl.ds(pl.multiple_of(lax.rem(t, 2) * big, big), big)

time: 197 us -> 193 us (0.980)
  Pallas kernels: 194 us -> 190 us
    pallas_call x1, Pallas kernels: 194 us -> 190 us  [local_step(): pl.pallas_call(attend_kernel, out_shape=(jax.ShapeDtypeStruct((n_batch *...]
where the time goes in v2:
time: 193 us; the launch traced here: 192 us
  Pallas kernels  190 us (98%)
  local copies, waits for them, and re-layouts  2.65 us (1%)
    pallas_call x1, Pallas kernels, local_step(): pl.pallas_call(attend_kernel, out_shape=(jax.ShapeDtypeStruct((n_batch *...  190 us

profile of v2, /device:TPU:0, one launch (start us, length us, event | category | flops | bytes accessed | tf_op | source)
XLA Modules:
  0.0 192.3 jit_solution(15161799316799025684)
XLA Ops:
  0.0 189.6 %shard_map.73 = (bf16[256,3072]{1,0:T(8,128)(2,1)}, f32[8,512,256]{2,1,0:T(8,128)}, f32[8,512,256]{2,1,0:T(8,128)}, bf16[8,512,256]{2,1,0:T(8,128)(2,1)}, bf16[8,512,256]{2,1,0:T(8,128)(2,1)}) custom-call(s32[4]{0:T(128)} %len_ref.1, bf16[4,64,3072]{2,1,0:T(8,128)(2,1)} %qin_hbm.1, bf16[4,512,3072]{2,1,0:T(8,128)(2,1)} %mem_hbm.1, ...), custom_call_target="tpu_custom_call" | custom-call | tf_op jit(solution)/shard_map/pallas_call | solution.py:425
  189.6 2.7 %copy.9 = bf16[4,64,3072]{2,1,0:T(8,128)(2,1)} copy(bf16[4,64,3072]{2,1,0:T(8,128)(2,1)} %bitcast.3) | data formatting | bytes 3145728

commit v3 on v2

--- a/solution.py
+++ b/solution.py
@@ -228,12 +228,12 @@
                 def _():
                     relayout((raw_k, raw_v)[j], w_next, j, t * part, part)
 
-                p = [weights(h_prev, t, i, kv_prev, k_prev) for i in range(2)]
                 side = lax.rem(core + t // 2, 2)
                 r = pl.ds(pl.multiple_of(lax.rem(t, 2) * big, big), big)
                 for sel in range(2):
+                    p = weights(h_prev, t, sel, kv_prev, k_prev)
                     kv_now[sel, side, r, :] = jnp.dot(x_buf[side, r, :], w_now[j, sel], preferred_element_type=F32).astype(BF16)
-                    weighted(p[sel], t, sel, kv_prev, k_prev)
+                    weighted(p, t, sel, kv_prev, k_prev)
 
                 @pl.when(h >= 1)
                 def _():

time: 193 us -> 196 us (1.016)
  Pallas kernels: 190 us -> 193 us
    pallas_call x1, Pallas kernels: 190 us -> 193 us  [local_step(): pl.pallas_call(attend_kernel, out_shape=(jax.ShapeDtypeStruct((n_batch *...]
where the time goes in v3:
time: 196 us
  Pallas kernels  193 us (98%)
  local copies, waits for them, and re-layouts  2.65 us (1%)
    pallas_call x1, Pallas kernels, local_step(): pl.pallas_call(attend_kernel, out_shape=(jax.ShapeDtypeStruct((n_batch *...  193 us

profile of v3, /device:TPU:0, one launch (start us, length us, event | category | flops | bytes accessed | tf_op | source)
XLA Modules:
  0.0 195.6 jit_solution(12401334430802117535)
XLA Ops:
  0.0 192.9 %shard_map.73 = (bf16[256,3072]{1,0:T(8,128)(2,1)}, f32[8,512,256]{2,1,0:T(8,128)}, f32[8,512,256]{2,1,0:T(8,128)}, bf16[8,512,256]{2,1,0:T(8,128)(2,1)}, bf16[8,512,256]{2,1,0:T(8,128)(2,1)}) custom-call(s32[4]{0:T(128)} %len_ref.1, bf16[4,64,3072]{2,1,0:T(8,128)(2,1)} %qin_hbm.1, bf16[4,512,3072]{2,1,0:T(8,128)(2,1)} %mem_hbm.1, ...), custom_call_target="tpu_custom_call" | custom-call | tf_op jit(solution)/shard_map/pallas_call | solution.py:425
  192.9 2.7 %copy.9 = bf16[4,64,3072]{2,1,0:T(8,128)(2,1)} copy(bf16[4,64,3072]{2,1,0:T(8,128)(2,1)} %bitcast.3) | data formatting | bytes 3145728
